TPU v7x, 32 devices: a whole 2x2x4 slice. The times are simulated.
32 devices in a mesh: gx: 4 (over y, x), gy: 2 (over core), gz: 4 (over z).
Axes of the slice: x: 2, y: 2, z: 4, core: 2. Of those that a mesh axis runs over, the one named last changes fastest.
Arguments:
- dual_operators: bfloat16 [4, 2, 4, 768, 768], P('gx', 'gy', 'gz'), may hold values from -1 to 3, as said below
- dual_load: float32 [4, 2, 4, 32, 384], P('gx', 'gy', 'gz'), may hold values from -25 to 25
- rigid_modes: float32 [4, 2, 4, 6, 768], P('gx', 'gy', 'gz'), may hold values from -0.21875 to 0.21875
- coarse_load: float32 [4, 2, 4, 6, 32], P('gx', 'gy', 'gz'), may hold values from -24 to 24
- mode_counts: int32 [4, 2, 4], P('gx', 'gy', 'gz'), may hold values from 3 to 6
- face_maps: int32 [4, 2, 4, 3, 128], P('gx', 'gy', 'gz'), may hold values from 0 to 127, each once within a row
Outputs:
- multipliers: float32 [4, 2, 4, 32, 384], P('gx', 'gy', 'gz')
- residual: float32 [4, 2, 4, 32, 384], P('gx', 'gy', 'gz')
Inputs may be any that keep to these rules, and one draw needn't show every extreme that they name: Each dual_operators[i, j, k] is symmetric positive definite. Subdomain s uses rows 0 to mode_counts[s] - 1 of rigid_modes[s]. Each face_maps[i, j, k, d] holds every number of 0 to 127 once.
All inputs are finite; a program needn't handle non-finite values.
Results may differ from a plain program's by a relative error of at most 0.012.
Values sent between devices are 32-bit elements; how exact they have to be, the bound alone decides.
A program may use at most 64 MiB of HBM per device.

v0:
```python
import functools

import jax
import jax.numpy as jnp
from jax import lax
from jax.experimental import pallas as pl
from jax.experimental.pallas import tpu as pltpu
from jax.sharding import PartitionSpec as P

MESH = pl.DeviceIdType.MESH
HIGH = lax.Precision.HIGHEST
NN = (((1,), (0,)), ((), ()))
NT = (((1,), (1,)), ((), ()))
TN = (((0,), (0,)), ((), ()))


def mul(a, b, dims=NN):
    return lax.dot_general(a, b, dims, precision=HIGH, preferred_element_type=jnp.float32)


def split(a):
    head = a.astype(jnp.bfloat16)
    return head, (a - head.astype(jnp.float32)).astype(jnp.bfloat16)


def fast(a, b, dims=NN):
    if dims == TN:
        a, dims = a.T, NN
    (ah, al), (bh, bl) = split(a), split(b)
    dot = functools.partial(
        lax.dot_general, dimension_numbers=dims, preferred_element_type=jnp.float32
    )
    return dot(ah, bh) + (dot(ah, bl) + dot(al, bh))


def eliminate(system, size, block=8):
    rows = lax.broadcasted_iota(jnp.int32, system.shape, 0)
    span = range(block)
    for k in range(0, size, block):
        columns = [system[:, k + j : k + j + 1] for j in span]
        lines = [system[k + i : k + i + 1, :] for i in span]
        pivots = [
            [jnp.broadcast_to(lines[i][:, k + j : k + j + 1], lines[i].shape) for j in span]
            for i in span
        ]
        for j in span:
            scale = 1.0 / pivots[j][j]
            lines[j] = lines[j] * scale
            pivots[j] = [p * scale for p in pivots[j]]
            for i in span:
                if i != j:
                    factor = pivots[i][j]
                    lines[i] = lines[i] - factor * lines[j]
                    pivots[i] = [p - factor * q for p, q in zip(pivots[i], pivots[j])]
        update = columns[0] * lines[0]
        for j in span[1:]:
            update = update + columns[j] * lines[j]
        system = system - update
        for j in span:
            system = jnp.where(rows == k + j, lines[j], system)
    return system[:, size:]


def identity(size):
    return (
        lax.broadcasted_iota(jnp.int32, (size, size), 0)
        == lax.broadcasted_iota(jnp.int32, (size, size), 1)
    ).astype(jnp.float32)


def packed(gram, width):
    groups = max(1, width // gram.shape[1])
    depth = gram.shape[0] // groups
    return jnp.concatenate([gram[g * depth : (g + 1) * depth] for g in range(groups)], axis=1)


def unpacked(tile, size):
    groups = max(1, tile.shape[1] // size)
    return jnp.concatenate([tile[:, g * size : (g + 1) * size] for g in range(groups)], axis=0)


def kernel(
    extents,
    operator_hbm,
    load_hbm,
    modes_hbm,
    coarse_hbm,
    count_ref,
    maps_hbm,
    multipliers_ref,
    residual_ref,
    raw,
    load_ref,
    modes_ref,
    coarse_ref,
    maps_ref,
    ordered,
    own_modes,
    all_modes,
    padded_load,
    probes,
    first_out,
    first_in,
    pair_out,
    pair_in,
    face_out,
    face_in,
    last_out,
    last_in,
    load_in,
    plane_sums,
    line_sums,
    raw_sem,
    first_send,
    first_recv,
    face_send,
    face_recv,
    pair_send,
    pair_recv,
    last_send,
    last_recv,
    load_send,
    load_recv,
    plane_send,
    plane_recv,
    line_send,
    line_recv,
):
    nx, ny, nz = extents
    cases = load_hbm.shape[0]
    width = load_hbm.shape[1] // 3
    modes = modes_hbm.shape[0]
    padded = own_modes.shape[0]
    here = (lax.axis_index("gx"), lax.axis_index("gy"), lax.axis_index("gz"))
    ix, iy, iz = here
    plane = nx * ny
    slot = ix * ny + iy

    fetches = [
        pltpu.make_async_copy(source, target, raw_sem.at[i])
        for i, (source, target) in enumerate(
            (
                (maps_hbm, maps_ref),
                (modes_hbm, modes_ref),
                (coarse_hbm, coarse_ref),
                (load_hbm, load_ref),
                (operator_hbm, raw),
            )
        )
    ]
    for fetch in fetches:
        fetch.start()

    all_modes[...] = jnp.zeros(all_modes.shape, jnp.float32)
    probes[...] = jnp.zeros(probes.shape, jnp.float32)
    first_in[...] = jnp.zeros(first_in.shape, jnp.float32)
    pair_in[...] = jnp.zeros(pair_in.shape, jnp.float32)
    pair_out[...] = jnp.zeros(pair_out.shape, jnp.float32)
    face_out[:, :, cases:, :] = jnp.zeros((2, 6, 2 * padded, width), jnp.float32)
    face_in[:, :, cases:, :] = jnp.zeros((2, 6, 2 * padded, width), jnp.float32)
    own_modes[...] = jnp.zeros(own_modes.shape, jnp.float32)
    padded_load[...] = jnp.zeros(padded_load.shape, jnp.float32)

    def plane_peer(offset):
        other = lax.rem(slot + offset, plane)
        return (lax.div(other, ny), lax.rem(other, ny), iz)

    def line_peer(offset):
        return (ix, iy, lax.rem(iz + offset, nz))

    exists = []
    neighbour = []
    for d in range(3):
        exists.append(here[d] > 0)
        exists.append(here[d] < extents[d] - 1)
        for step in (-1, 1):
            neighbour.append(tuple(here[a] + (step if a == d else 0) for a in range(3)))
    flags = [jnp.where(e, 1, 0).astype(jnp.int32) for e in exists]

    def moved(position, f):
        return tuple(position[a] + ((2 * (f % 2) - 1) if a == f // 2 else 0) for a in range(3))

    def both_exist(f, g):
        if f != g:
            return jnp.logical_and(exists[f], exists[g])
        if f % 2:
            return here[f // 2] < extents[f // 2] - 2
        return here[f // 2] > 1

    pairs = [
        (f, g)
        for f in range(6)
        for g in range(6)
        if (f == g or f // 2 < g // 2) and extents[f // 2] > 1 + (f == g) and extents[g // 2] > 1
    ]

    barrier = pltpu.get_barrier_semaphore()
    diagonal = 0
    for f in range(4):
        for g in range(4, 6):
            peer = moved(moved(here, f), g)

            @pl.when(both_exist(f, g))
            def _(peer=peer):
                pl.semaphore_signal(barrier, inc=1, device_id=peer, device_id_type=MESH)

            diagonal = diagonal + flags[f] * flags[g]
    for offset in range(1, plane):
        pl.semaphore_signal(barrier, inc=1, device_id=plane_peer(offset), device_id_type=MESH)
    for offset in range(1, nz):
        pl.semaphore_signal(barrier, inc=1, device_id=line_peer(offset), device_id_type=MESH)


    def face(values, f):
        return values[:, f * width : (f + 1) * width]

    def masked(values, f):
        return jnp.where(jnp.full(values.shape, flags[f], jnp.int32) == 1, values, 0.0)

    sends = [[] for _ in range(6)]
    pair_sends = [[] for _ in pairs]

    def remote(source, target, send, recv, where):
        return pltpu.make_async_remote_copy(
            src_ref=source,
            dst_ref=target,
            send_sem=send,
            recv_sem=recv,
            device_id=where,
            device_id_type=MESH,
        )

    def start_to(f, copies):
        @pl.when(exists[f])
        def _():
            for copy in copies:
                copy.start()

        sends[f].extend(copies)

    for fetch in fetches[:4]:
        fetch.wait()
    count = count_ref[0, 0]
    lines = lax.broadcasted_iota(jnp.int32, (width, width), 0)
    orders = [(lines == maps_ref[d]).astype(jnp.float32) for d in range(3)]
    for m in range(modes):
        own_modes[m : m + 1, :] = modes_ref[m]
        padded_load[m : m + 1, 0:cases] = coarse_ref[m]
    raw_modes = jnp.where(
        lax.broadcasted_iota(jnp.int32, own_modes.shape, 0) < count, own_modes[...], 0.0
    )
    pieces = []
    for d in range(3):
        pieces.append(masked(mul(face(raw_modes, 2 * d), orders[d], NT), 2 * d))
        pieces.append(masked(face(raw_modes, 2 * d + 1), 2 * d + 1))
    mode_rows = jnp.concatenate(pieces, axis=1)
    own_modes[...] = mode_rows
    all_modes[0:padded, :] = mode_rows
    inactive = lax.broadcasted_iota(jnp.int32, (padded, padded), 0) >= count
    normal = mul(mode_rows, mode_rows, NT) + jnp.where(inactive, identity(padded), 0.0)
    coarse_inverse = eliminate(jnp.concatenate([normal, identity(padded)], axis=1), padded)
    active_load = jnp.where(
        lax.broadcasted_iota(jnp.int32, padded_load.shape, 0) < count, padded_load[...], 0.0
    )
    first_part = mul(coarse_inverse, active_load)
    inverse_modes = mul(coarse_inverse, mode_rows)
    probes[6 * padded :, :] = inverse_modes
    for f in range(6):
        first_out[f, 0:padded, :] = -face(mode_rows, f)
        first_out[f, padded : 2 * padded, :] = face(inverse_modes, f)
        first_out[f, 2 * padded :, :] = first_part

    pl.semaphore_wait(barrier, plane - 1 + nz - 1 + diagonal)

    for f in range(6):
        copies = [
            remote(first_out.at[f], first_in.at[f ^ 1], first_send.at[f], first_recv.at[f ^ 1], neighbour[f])
        ]
        if f % 2:
            d = f // 2
            copies.append(
                remote(
                    load_ref.at[:, pl.ds(d * width, width)],
                    load_in.at[d],
                    load_send.at[d],
                    load_recv.at[d],
                    neighbour[f],
                )
            )
        start_to(f, copies)

    def send_round(phase, values, own=None):
        found = fast(probes[...], values, NT)
        share = found[6 * padded :] if own is None else own - found[6 * padded :]
        for f in range(6):
            face_out[phase, f, 0:cases, :] = face(values, f)
            face_out[phase, f, cases : cases + padded, 0:cases] = share
            face_out[phase, f, cases + padded :, 0:cases] = found[f * padded : (f + 1) * padded]
        for index, (f, g) in enumerate(pairs):
            pair_out[phase, index, 0:padded, 0:cases] = found[f * padded : (f + 1) * padded]
            if f != g:
                pair_out[phase, index, padded:, 0:cases] = found[g * padded : (g + 1) * padded]
        for index, (f, g) in enumerate(pairs):
            other = pairs.index((f ^ 1, g ^ 1))
            copy = remote(
                pair_out.at[phase, index],
                pair_in.at[phase, other],
                pair_send.at[phase, index],
                pair_recv.at[phase, other],
                moved(moved(here, f), g),
            )
            pl.when(both_exist(f, g))(copy.start)
            pair_sends[index].append(copy)
        for f in range(6):
            start_to(
                f,
                [
                    remote(
                        face_out.at[phase, f],
                        face_in.at[phase, f ^ 1],
                        face_send.at[phase, f],
                        face_recv.at[phase, f ^ 1],
                        neighbour[f],
                    )
                ],
            )
        return found, share

    def wait_faces(phase, source, target, send, recv):
        for f in range(6):
            copy = remote(
                source.at[phase, f], target.at[phase, f], send.at[phase, f], recv.at[phase, f], neighbour[f]
            )
            pl.when(exists[f])(copy.wait_recv)

    def wait_pairs(phase):
        for index, (f, g) in enumerate(pairs):
            copy = remote(
                pair_out.at[phase, index],
                pair_in.at[phase, index],
                pair_send.at[phase, index],
                pair_recv.at[phase, index],
                moved(moved(here, f), g),
            )
            pl.when(both_exist(f, g))(copy.wait_recv)

    def assembled(mine, theirs, phase):
        return jnp.concatenate(
            [
                masked(mine[phase, f, 0:cases, :] - theirs[phase, f, 0:cases, :], f)
                for f in range(6)
            ],
            axis=1,
        )

    def apply_local(values):
        head = values.astype(jnp.bfloat16)
        tail = (values - head.astype(jnp.float32)).astype(jnp.bfloat16)
        both = jnp.dot(
            jnp.concatenate([head, tail], axis=0),
            ordered[...],
            preferred_element_type=jnp.float32,
        )
        return both[0:cases] + both[cases:]

    def owned(values):
        return jnp.concatenate([face(values, 1), face(values, 3), face(values, 5)], axis=1)

    fetches[4].wait()
    narrow = [order.astype(jnp.bfloat16) for order in orders]
    for d in range(3):
        low = 2 * d * width
        raw[pl.ds(low, width), :] = jnp.dot(
            narrow[d], raw[pl.ds(low, width), :], preferred_element_type=jnp.float32
        ).astype(jnp.bfloat16)
    for d in range(3):
        low = 2 * d * width
        ordered[:, low : low + width] = lax.dot_general(
            raw[:, low : low + width], narrow[d], NT, preferred_element_type=jnp.float32
        ).astype(jnp.bfloat16)
        ordered[:, low + width : low + 2 * width] = raw[:, low + width : low + 2 * width]
    for f in range(6):
        d = f // 2
        first = remote(first_out.at[f], first_in.at[f], first_send.at[f], first_recv.at[f], neighbour[f])
        pl.when(exists[f])(first.wait_recv)
    coefficients = [first_part]
    for f in range(6):
        all_modes[(1 + f) * padded : (2 + f) * padded, f * width : (f + 1) * width] = first_in[
            f, 0:padded, :
        ]
        probes[f * padded : (f + 1) * padded, f * width : (f + 1) * width] = first_in[
            f, padded : 2 * padded, :
        ]
        coefficients.append(first_in[f, 2 * padded :, :])
    initial = fast(jnp.concatenate(coefficients, axis=0)[:, 0:cases], all_modes[...], TN)
    product = apply_local(initial)
    right = []
    for d in range(3):
        copy = remote(
            load_ref.at[:, pl.ds(d * width, width)],
            load_in.at[d],
            load_send.at[d],
            load_recv.at[d],
            neighbour[2 * d],
        )
        pl.when(exists[2 * d])(copy.wait_recv)
    for d in range(3):
        right.append(masked(-load_in[d], 2 * d))
        right.append(masked(load_ref[:, d * width : (d + 1) * width], 2 * d + 1))
    right = jnp.concatenate(right, axis=1)
    shares = send_round(0, product, fast(inverse_modes, right, NT))
    wait_faces(0, face_out, face_in, face_send, face_recv)
    residual = right - assembled(face_out, face_in, 0)

    def preconditioned(phase, values, shares, sign):
        found, own = shares
        back = face_in[phase, 0, cases + padded :, 0:cases]
        for f in range(1, 6):
            back = back + face_in[phase, f, cases + padded :, 0:cases]
        own = own - sign * back
        wait_pairs(phase)
        terms = [found[f * padded : (f + 1) * padded] for f in range(6)]
        for index, (a, b) in enumerate(pairs):
            terms[b] = terms[b] + pair_in[phase, index, 0:padded, 0:cases]
            if a != b:
                terms[a] = terms[a] + pair_in[phase, index, padded:, 0:cases]
        every = [own]
        for f in range(6):
            every.append(face_in[phase, f, cases : cases + padded, 0:cases] - sign * terms[f])
        return values - 0.25 * fast(jnp.concatenate(every, axis=0), all_modes[...], TN)

    def sum_start(which, tile):
        plane_sums[which, slot] = tile
        copies = []
        for offset in range(1, plane):
            copy = remote(
                plane_sums.at[which, slot],
                plane_sums.at[which, slot],
                plane_send.at[which, offset],
                plane_recv.at[which, offset],
                plane_peer(offset),
            )
            copy.start()
            copies.append(copy)
        return copies

    def sum_middle(which, copies):
        for offset in range(1, plane):
            copy = remote(
                plane_sums.at[which, slot],
                plane_sums.at[which, lax.rem(slot + plane - offset, plane)],
                plane_send.at[which, offset],
                plane_recv.at[which, offset],
                plane_peer(offset),
            )
            copy.wait_recv()
        total = plane_sums[which, 0]
        for other in range(1, plane):
            total = total + plane_sums[which, other]
        line_sums[which, iz] = total
        for offset in range(1, nz):
            copy = remote(
                line_sums.at[which, iz],
                line_sums.at[which, iz],
                line_send.at[which, offset],
                line_recv.at[which, offset],
                line_peer(offset),
            )
            copy.start()
            copies.append(copy)

    def sum_end(which):
        for offset in range(1, nz):
            copy = remote(
                line_sums.at[which, iz],
                line_sums.at[which, lax.rem(iz + nz - offset, nz)],
                line_send.at[which, offset],
                line_recv.at[which, offset],
                line_peer(offset),
            )
            copy.wait_recv()
        total = line_sums[which, 0]
        for other in range(1, nz):
            total = total + line_sums[which, other]
        half = total.shape[0] // 2
        return unpacked(total[0:half], cases), unpacked(total[half:], cases)

    start = preconditioned(0, residual, shares, -1.0)
    product = apply_local(start)
    shares = send_round(1, product)
    early = sum_start(
        0,
        jnp.concatenate(
            [
                packed(fast(owned(start), owned(residual), NT), width),
                packed(fast(start, product, NT), width),
            ],
            axis=0,
        ),
    )
    wait_faces(1, face_out, face_in, face_send, face_recv)
    image = assembled(face_out, face_in, 1)
    sum_middle(0, early)
    second = preconditioned(1, image, shares, 1.0)
    product = apply_local(second)
    late = sum_start(
        1,
        jnp.concatenate(
            [
                packed(fast(owned(second), owned(image), NT), width),
                packed(fast(second, product, NT), width),
            ],
            axis=0,
        ),
    )
    for f in range(6):
        last_out[0, f] = face(product, f)
    for f in range(6):
        start_to(
            f,
            [
                remote(
                    last_out.at[0, f],
                    last_in.at[0, f ^ 1],
                    last_send.at[0, f],
                    last_recv.at[0, f ^ 1],
                    neighbour[f],
                )
            ],
        )
    gram, energy = sum_end(0)
    inverse = eliminate(jnp.concatenate([energy, identity(cases)], axis=1), cases)
    alpha = fast(inverse, gram)
    sum_middle(1, late)
    wait_faces(0, last_out, last_in, last_send, last_recv)
    second_image = assembled(last_out, last_in, 0)
    cross, last = sum_end(1)
    carried = fast(inverse, cross)
    schur = last - fast(cross, carried)
    right_side = fast(cross, alpha) - energy
    tail = eliminate(jnp.concatenate([schur, right_side], axis=1), cases)
    head = alpha + fast(carried, tail)
    both = jnp.concatenate([head, -tail], axis=0)
    multipliers_ref[...] = owned(initial) + fast(
        both, jnp.concatenate([owned(start), owned(second)], axis=0), TN
    )
    residual_ref[...] = owned(residual) - fast(
        both, jnp.concatenate([owned(image), owned(second_image)], axis=0), TN
    )

    def finish(condition, copies):
        @pl.when(condition)
        def _():
            for copy in copies:
                copy.wait_send()

    for f in range(6):
        finish(exists[f], sends[f])
    for index, (f, g) in enumerate(pairs):
        finish(both_exist(f, g), pair_sends[index])
    for copy in early + late:
        copy.wait_send()


def held(array):
    return pltpu.with_memory_space_constraint(array, pltpu.HBM)


def rows_apart(array):
    return jnp.swapaxes(array, 2, 3).reshape(array.shape[3], 1, array.shape[4])


def local(extents, dual_operators, dual_load, rigid_modes, coarse_load, mode_counts, face_maps):
    size = dual_operators.shape[-1]
    cases = dual_load.shape[-2]
    width = dual_load.shape[-1] // 3
    modes = rigid_modes.shape[-2]
    padded = -(-modes // 8) * 8
    nx, ny, nz = extents
    plane = nx * ny
    tile = 2 * cases // max(1, width // cases)
    f32 = jnp.float32
    vmem = pl.BlockSpec(memory_space=pltpu.VMEM)
    hbm = pl.BlockSpec(memory_space=pltpu.HBM)
    dma = pltpu.SemaphoreType.DMA
    out = jax.ShapeDtypeStruct((cases, 3 * width), f32)
    multipliers, residual = pl.pallas_call(
        functools.partial(kernel, extents),
        out_shape=(out, out),
        in_specs=[
            hbm,
            hbm,
            hbm,
            hbm,
            pl.BlockSpec(memory_space=pltpu.SMEM),
            hbm,
        ],
        out_specs=(vmem, vmem),
        scratch_shapes=[
            pltpu.VMEM((size, size), dual_operators.dtype),
            pltpu.VMEM((cases, 3 * width), f32),
            pltpu.VMEM((modes, 1, size), f32),
            pltpu.VMEM((modes, 1, cases), f32),
            pltpu.VMEM((3, 1, width), jnp.int32),
            pltpu.VMEM((size, size), dual_operators.dtype),
            pltpu.VMEM((padded, size), f32),
            pltpu.VMEM((7 * padded, size), f32),
            pltpu.VMEM((padded, width), f32),
            pltpu.VMEM((7 * padded, size), f32),
            pltpu.VMEM((6, 3 * padded, width), f32),
            pltpu.VMEM((6, 3 * padded, width), f32),
            pltpu.VMEM((2, 18, 2 * padded, width), f32),
            pltpu.VMEM((2, 18, 2 * padded, width), f32),
            pltpu.VMEM((2, 6, cases + 2 * padded, width), f32),
            pltpu.VMEM((2, 6, cases + 2 * padded, width), f32),
            pltpu.VMEM((1, 6, cases, width), f32),
            pltpu.VMEM((1, 6, cases, width), f32),
            pltpu.VMEM((3, cases, width), f32),
            pltpu.VMEM((2, plane, tile, width), f32),
            pltpu.VMEM((2, nz, tile, width), f32),
            dma((5,)),
            dma((6,)),
            dma((6,)),
            dma((2, 6)),
            dma((2, 6)),
            dma((2, 18)),
            dma((2, 18)),
            dma((1, 6)),
            dma((1, 6)),
            dma((3,)),
            dma((3,)),
            dma((2, plane)),
            dma((2, plane)),
            dma((2, nz)),
            dma((2, nz)),
        ],
        compiler_params=pltpu.CompilerParams(collective_id=0, has_side_effects=True, vmem_limit_bytes=16 * 1024 * 1024
        ),
    )(
        held(dual_operators.reshape(size, size)),
        held(dual_load.reshape(cases, 3 * width)),
        held(rows_apart(rigid_modes)),
        held(rows_apart(coarse_load)),
        mode_counts.reshape(1, 1),
        held(rows_apart(face_maps)),
    )
    shape = (1, 1, 1, cases, 3 * width)
    return multipliers.reshape(shape), residual.reshape(shape)


def solution(mesh):
    extents = (mesh.shape["gx"], mesh.shape["gy"], mesh.shape["gz"])
    spec = P("gx", "gy", "gz", None, None)
    return jax.shard_map(
        functools.partial(local, extents),
        mesh=mesh,
        in_specs=(spec, spec, spec, spec, P("gx", "gy", "gz"), spec),
        out_specs=(spec, spec),
        check_vma=False,
    )
```

profile of v0, /device:TPU:0, one launch (start us, length us, event | category | flops | bytes accessed | tf_op | source)
XLA Modules:
  0.0 32.8 jit_solution(17473142532335491969)
XLA Ops:
  1.3 30.3 %shard_map.77 = (f32[32,384]{1,0:T(8,128)S(1)}, f32[32,384]{1,0:T(8,128)S(1)}) custom-call(bf16[768,768]{1,0:T(8,128)(2,1)} %bitcast.11, f32[32,384]{1,0:T(8,128)} %bitcast.12, f32[6,1,768]{2,1,0:T(1,128)} %bitcast.13, f32[6,1,32]{2,1,0:T(1,128)} %bitcast.14, s32[1,1]{1,0:T(1,128)} %bitcast.8.count_ref, s32[3,1,128]{2,1,0:T(1,128)} %bitcast.15), custom_call_target="tpu_custom_call" | custom-call | tf_op jit(solution)/shard_map/pallas_call | solution.py:587
  31.6 0.6 %copy.11 = f32[1,1,1,32,384]{4,3,2,1,0:T(8,128)} copy(f32[1,1,1,32,384]{4,3,2,1,0:T(8,128)S(1)} %bitcast.10) | data formatting | bytes 98304
  32.2 0.6 %copy.12 = f32[1,1,1,32,384]{4,3,2,1,0:T(8,128)} copy(f32[1,1,1,32,384]{4,3,2,1,0:T(8,128)S(1)} %bitcast.9) | data formatting | bytes 98304
where the time goes:
time: 33 us; the launch traced here: 32.8 us
  Pallas kernels  30.3 us (92%)
  between operations  1.29 us (4%)
  local copies, waits for them, and re-layouts  1.24 us (4%)
    pallas_call x1, Pallas kernels, local(): pl.pallas_call(functools.partial(kernel, extents), out_shape=(out, out),...  30.3 us
    unnamed x2, local copies, waits for them, and re-layouts  1.24 us

commit v1 on v0

--- a/solution.py
+++ b/solution.py
@@ -85,7 +85,7 @@
     load_hbm,
     modes_hbm,
     coarse_hbm,
-    count_ref,
+    count_hbm,
     maps_hbm,
     multipliers_ref,
     residual_ref,
@@ -94,6 +94,7 @@
     modes_ref,
     coarse_ref,
     maps_ref,
+    count_ref,
     ordered,
     own_modes,
     all_modes,
@@ -140,6 +141,7 @@
         pltpu.make_async_copy(source, target, raw_sem.at[i])
         for i, (source, target) in enumerate(
             (
+                (count_hbm, count_ref),
                 (maps_hbm, maps_ref),
                 (modes_hbm, modes_ref),
                 (coarse_hbm, coarse_ref),
@@ -151,22 +153,14 @@
     for fetch in fetches:
         fetch.start()
 
-    all_modes[...] = jnp.zeros(all_modes.shape, jnp.float32)
-    probes[...] = jnp.zeros(probes.shape, jnp.float32)
-    first_in[...] = jnp.zeros(first_in.shape, jnp.float32)
-    pair_in[...] = jnp.zeros(pair_in.shape, jnp.float32)
-    pair_out[...] = jnp.zeros(pair_out.shape, jnp.float32)
-    face_out[:, :, cases:, :] = jnp.zeros((2, 6, 2 * padded, width), jnp.float32)
-    face_in[:, :, cases:, :] = jnp.zeros((2, 6, 2 * padded, width), jnp.float32)
-    own_modes[...] = jnp.zeros(own_modes.shape, jnp.float32)
-    padded_load[...] = jnp.zeros(padded_load.shape, jnp.float32)
-
     def plane_peer(offset):
         other = lax.rem(slot + offset, plane)
         return (lax.div(other, ny), lax.rem(other, ny), iz)
 
-    def line_peer(offset):
-        return (ix, iy, lax.rem(iz + offset, nz))
+    def line_peers():
+        for turn in range(ny):
+            for offset in range(1, nz):
+                yield (ix, lax.rem(iy + turn, ny), lax.rem(iz + offset, nz))
 
     exists = []
     neighbour = []
@@ -194,6 +188,10 @@
         if (f == g or f // 2 < g // 2) and extents[f // 2] > 1 + (f == g) and extents[g // 2] > 1
     ]
 
+    first_in[...] = jnp.zeros(first_in.shape, jnp.float32)
+    pair_in[...] = jnp.zeros(pair_in.shape, jnp.float32)
+    face_in[:, :, cases:, :] = jnp.zeros((2, 6, 2 * padded, width), jnp.float32)
+
     barrier = pltpu.get_barrier_semaphore()
     diagonal = 0
     for f in range(4):
@@ -207,9 +205,15 @@
             diagonal = diagonal + flags[f] * flags[g]
     for offset in range(1, plane):
         pl.semaphore_signal(barrier, inc=1, device_id=plane_peer(offset), device_id_type=MESH)
-    for offset in range(1, nz):
-        pl.semaphore_signal(barrier, inc=1, device_id=line_peer(offset), device_id_type=MESH)
-
+    for peer in line_peers():
+        pl.semaphore_signal(barrier, inc=1, device_id=peer, device_id_type=MESH)
+
+    all_modes[...] = jnp.zeros(all_modes.shape, jnp.float32)
+    probes[...] = jnp.zeros(probes.shape, jnp.float32)
+    pair_out[...] = jnp.zeros(pair_out.shape, jnp.float32)
+    face_out[:, :, cases:, :] = jnp.zeros((2, 6, 2 * padded, width), jnp.float32)
+    own_modes[...] = jnp.zeros(own_modes.shape, jnp.float32)
+    padded_load[...] = jnp.zeros(padded_load.shape, jnp.float32)
 
     def face(values, f):
         return values[:, f * width : (f + 1) * width]
@@ -238,16 +242,18 @@
 
         sends[f].extend(copies)
 
-    for fetch in fetches[:4]:
+    for fetch in fetches[:5]:
         fetch.wait()
-    count = count_ref[0, 0]
+    def counted(shape):
+        return jnp.broadcast_to(count_ref[...], shape)
+
     lines = lax.broadcasted_iota(jnp.int32, (width, width), 0)
     orders = [(lines == maps_ref[d]).astype(jnp.float32) for d in range(3)]
     for m in range(modes):
         own_modes[m : m + 1, :] = modes_ref[m]
         padded_load[m : m + 1, 0:cases] = coarse_ref[m]
     raw_modes = jnp.where(
-        lax.broadcasted_iota(jnp.int32, own_modes.shape, 0) < count, own_modes[...], 0.0
+        lax.broadcasted_iota(jnp.int32, own_modes.shape, 0) < counted(own_modes.shape), own_modes[...], 0.0
     )
     pieces = []
     for d in range(3):
@@ -256,11 +262,11 @@
     mode_rows = jnp.concatenate(pieces, axis=1)
     own_modes[...] = mode_rows
     all_modes[0:padded, :] = mode_rows
-    inactive = lax.broadcasted_iota(jnp.int32, (padded, padded), 0) >= count
+    inactive = lax.broadcasted_iota(jnp.int32, (padded, padded), 0) >= counted((padded, padded))
     normal = mul(mode_rows, mode_rows, NT) + jnp.where(inactive, identity(padded), 0.0)
     coarse_inverse = eliminate(jnp.concatenate([normal, identity(padded)], axis=1), padded)
     active_load = jnp.where(
-        lax.broadcasted_iota(jnp.int32, padded_load.shape, 0) < count, padded_load[...], 0.0
+        lax.broadcasted_iota(jnp.int32, padded_load.shape, 0) < counted(padded_load.shape), padded_load[...], 0.0
     )
     first_part = mul(coarse_inverse, active_load)
     inverse_modes = mul(coarse_inverse, mode_rows)
@@ -270,7 +276,7 @@
         first_out[f, padded : 2 * padded, :] = face(inverse_modes, f)
         first_out[f, 2 * padded :, :] = first_part
 
-    pl.semaphore_wait(barrier, plane - 1 + nz - 1 + diagonal)
+    pl.semaphore_wait(barrier, plane - 1 + ny * (nz - 1) + diagonal)
 
     for f in range(6):
         copies = [
@@ -366,7 +372,7 @@
     def owned(values):
         return jnp.concatenate([face(values, 1), face(values, 3), face(values, 5)], axis=1)
 
-    fetches[4].wait()
+    fetches[5].wait()
     narrow = [order.astype(jnp.bfloat16) for order in orders]
     for d in range(3):
         low = 2 * d * width
@@ -429,66 +435,93 @@
             every.append(face_in[phase, f, cases : cases + padded, 0:cases] - sign * terms[f])
         return values - 0.25 * fast(jnp.concatenate(every, axis=0), all_modes[...], TN)
 
+    relay = ny - 1
+    is_relay = iy == relay
+
+    def gather_copy(which, offset):
+        other = lax.rem(ix + offset, nx)
+        return remote(
+            plane_sums.at[which, slot],
+            plane_sums.at[which, slot],
+            plane_send.at[which, offset],
+            plane_recv.at[which, slot],
+            (other, relay, iz),
+        )
+
+    def spread_targets():
+        for turn in range(ny):
+            for offset in range(nz):
+                if turn or offset:
+                    yield turn * nz + offset, (lax.rem(relay + turn, ny), lax.rem(iz + offset, nz))
+
+    def spread_copy(which, index, position):
+        return remote(
+            line_sums.at[which, iz],
+            line_sums.at[which, iz],
+            line_send.at[which, index],
+            line_recv.at[which, iz],
+            (ix, *position),
+        )
+
     def sum_start(which, tile):
         plane_sums[which, slot] = tile
-        copies = []
-        for offset in range(1, plane):
+        for offset in range(nx):
+            if offset:
+                gather_copy(which, offset).start()
+            else:
+                pl.when(iy != relay)(gather_copy(which, offset).start)
+
+    def sum_middle(which):
+        @pl.when(is_relay)
+        def _():
+            for other in range(plane):
+                copy = remote(
+                    plane_sums.at[which, other],
+                    plane_sums.at[which, other],
+                    plane_send.at[which, 0],
+                    plane_recv.at[which, other],
+                    (ix, iy, iz),
+                )
+                pl.when(slot != other)(copy.wait_recv)
+            total = plane_sums[which, 0]
+            for other in range(1, plane):
+                total = total + plane_sums[which, other]
+            line_sums[which, iz] = total
+            for index, position in spread_targets():
+                spread_copy(which, index, position).start()
+
+    def sum_end(which):
+        for other in range(nz):
             copy = remote(
-                plane_sums.at[which, slot],
-                plane_sums.at[which, slot],
-                plane_send.at[which, offset],
-                plane_recv.at[which, offset],
-                plane_peer(offset),
+                line_sums.at[which, other],
+                line_sums.at[which, other],
+                line_send.at[which, 0],
+                line_recv.at[which, other],
+                (ix, iy, iz),
             )
-            copy.start()
-            copies.append(copy)
-        return copies
-
-    def sum_middle(which, copies):
-        for offset in range(1, plane):
-            copy = remote(
-                plane_sums.at[which, slot],
-                plane_sums.at[which, lax.rem(slot + plane - offset, plane)],
-                plane_send.at[which, offset],
-                plane_recv.at[which, offset],
-                plane_peer(offset),
-            )
-            copy.wait_recv()
-        total = plane_sums[which, 0]
-        for other in range(1, plane):
-            total = total + plane_sums[which, other]
-        line_sums[which, iz] = total
-        for offset in range(1, nz):
-            copy = remote(
-                line_sums.at[which, iz],
-                line_sums.at[which, iz],
-                line_send.at[which, offset],
-                line_recv.at[which, offset],
-                line_peer(offset),
-            )
-            copy.start()
-            copies.append(copy)
-
-    def sum_end(which):
-        for offset in range(1, nz):
-            copy = remote(
-                line_sums.at[which, iz],
-                line_sums.at[which, lax.rem(iz + nz - offset, nz)],
-                line_send.at[which, offset],
-                line_recv.at[which, offset],
-                line_peer(offset),
-            )
-            copy.wait_recv()
+            pl.when(jnp.logical_or(iy != relay, iz != other))(copy.wait_recv)
         total = line_sums[which, 0]
         for other in range(1, nz):
             total = total + line_sums[which, other]
         half = total.shape[0] // 2
         return unpacked(total[0:half], cases), unpacked(total[half:], cases)
 
+    def sum_finish(which):
+        for offset in range(nx):
+            if offset:
+                gather_copy(which, offset).wait_send()
+            else:
+                pl.when(iy != relay)(gather_copy(which, offset).wait_send)
+
+        @pl.when(is_relay)
+        def _():
+            for index, position in spread_targets():
+                spread_copy(which, index, position).wait_send()
+
     start = preconditioned(0, residual, shares, -1.0)
     product = apply_local(start)
     shares = send_round(1, product)
-    early = sum_start(
+    sum_start(
         0,
         jnp.concatenate(
             [
@@ -500,10 +533,10 @@
     )
     wait_faces(1, face_out, face_in, face_send, face_recv)
     image = assembled(face_out, face_in, 1)
-    sum_middle(0, early)
+    sum_middle(0)
     second = preconditioned(1, image, shares, 1.0)
     product = apply_local(second)
-    late = sum_start(
+    sum_start(
         1,
         jnp.concatenate(
             [
@@ -528,10 +561,10 @@
                 )
             ],
         )
+    sum_middle(1)
     gram, energy = sum_end(0)
     inverse = eliminate(jnp.concatenate([energy, identity(cases)], axis=1), cases)
     alpha = fast(inverse, gram)
-    sum_middle(1, late)
     wait_faces(0, last_out, last_in, last_send, last_recv)
     second_image = assembled(last_out, last_in, 0)
     cross, last = sum_end(1)
@@ -558,8 +591,19 @@
         finish(exists[f], sends[f])
     for index, (f, g) in enumerate(pairs):
         finish(both_exist(f, g), pair_sends[index])
-    for copy in early + late:
-        copy.wait_send()
+    for which in range(2):
+        sum_finish(which)
+
+
+def put_out(multipliers_ref, residual_ref, multipliers_hbm, residual_hbm, sem):
+    copies = [
+        pltpu.make_async_copy(multipliers_ref, multipliers_hbm, sem.at[0]),
+        pltpu.make_async_copy(residual_ref, residual_hbm, sem.at[1]),
+    ]
+    for copy in copies:
+        copy.start()
+    for copy in copies:
+        copy.wait()
 
 
 def held(array):
@@ -592,7 +636,7 @@
             hbm,
             hbm,
             hbm,
-            pl.BlockSpec(memory_space=pltpu.SMEM),
+            hbm,
             hbm,
         ],
         out_specs=(vmem, vmem),
@@ -602,6 +646,7 @@
             pltpu.VMEM((modes, 1, size), f32),
             pltpu.VMEM((modes, 1, cases), f32),
             pltpu.VMEM((3, 1, width), jnp.int32),
+            pltpu.VMEM((1, 1), jnp.int32),
             pltpu.VMEM((size, size), dual_operators.dtype),
             pltpu.VMEM((padded, size), f32),
             pltpu.VMEM((7 * padded, size), f32),
@@ -618,7 +663,7 @@
             pltpu.VMEM((3, cases, width), f32),
             pltpu.VMEM((2, plane, tile, width), f32),
             pltpu.VMEM((2, nz, tile, width), f32),
-            dma((5,)),
+            dma((6,)),
             dma((6,)),
             dma((6,)),
             dma((2, 6)),
@@ -629,9 +674,9 @@
             dma((1, 6)),
             dma((3,)),
             dma((3,)),
+            dma((2, nx)),
             dma((2, plane)),
-            dma((2, plane)),
-            dma((2, nz)),
+            dma((2, ny * nz)),
             dma((2, nz)),
         ],
         compiler_params=pltpu.CompilerParams(collective_id=0, has_side_effects=True, vmem_limit_bytes=16 * 1024 * 1024
@@ -644,6 +689,14 @@
         mode_counts.reshape(1, 1),
         held(rows_apart(face_maps)),
     )
+    multipliers, residual = pl.pallas_call(
+        put_out,
+        out_shape=(out, out),
+        in_specs=[vmem, vmem],
+        out_specs=(hbm, hbm),
+        scratch_shapes=[dma((2,))],
+        compiler_params=pltpu.CompilerParams(vmem_limit_bytes=1024 * 1024),
+    )(multipliers, residual)
     shape = (1, 1, 1, cases, 3 * width)
     return multipliers.reshape(shape), residual.reshape(shape)
 

time: 33 us -> 30.7 us (0.930)
  local copies, waits for them, and re-layouts: 1.24 us -> 0 us
  Pallas kernels: 30.3 us -> 29.3 us
    pallas_call x1, Pallas kernels: 30.3 us -> 28.6 us  [local(): pl.pallas_call(functools.partial(kernel, extents), out_shape=(out, out),...]
    unnamed x2 -> x0, local copies, waits for them, and re-layouts: 1.24 us -> none
    pallas_call x0 -> x1, Pallas kernels: none -> 0.66 us  [local(): pl.pallas_call(put_out, out_shape=(out, out), in_specs=[vmem, vmem], out_...]
where the time goes in v1:
time: 30.7 us; the launch traced here: 30.6 us
  Pallas kernels  29.3 us (95%)
  between operations  1.29 us (4%)
    pallas_call x1, Pallas kernels, local(): pl.pallas_call(functools.partial(kernel, extents), out_shape=(out, out),...  28.6 us
    pallas_call x1, Pallas kernels, local(): pl.pallas_call(put_out, out_shape=(out, out), in_specs=[vmem, vmem], out_...  0.66 us

profile of v1, /device:TPU:0, one launch (start us, length us, event | category | flops | bytes accessed | tf_op | source)
XLA Modules:
  0.0 30.6 jit_solution(3973275636189166318)
XLA Ops:
  1.3 28.6 %shard_map.77 = (f32[32,384]{1,0:T(8,128)S(1)}, f32[32,384]{1,0:T(8,128)S(1)}) custom-call(bf16[768,768]{1,0:T(8,128)(2,1)} %bitcast.9, f32[32,384]{1,0:T(8,128)} %bitcast.10, f32[6,1,768]{2,1,0:T(1,128)} %bitcast.11, f32[6,1,32]{2,1,0:T(1,128)} %bitcast.12, s32[1,1]{1,0:T(1,128)} %bitcast.8.count_hbm, s32[3,1,128]{2,1,0:T(1,128)} %bitcast.13), custom_call_target="tpu_custom_call" | custom-call | tf_op jit(solution)/shard_map/pallas_call | solution.py:631
  29.9 0.7 %shard_map.78 = (f32[32,384]{1,0:T(8,128)}, f32[32,384]{1,0:T(8,128)}) custom-call(f32[32,384]{1,0:T(8,128)S(1)} %get-tuple-element.6.multipliers_ref, f32[32,384]{1,0:T(8,128)S(1)} %get-tuple-element.7.residual_ref), custom_call_target="tpu_custom_call" | custom-call | tf_op jit(solution)/shard_map/pallas_call | solution.py:692

commit v2 on v1

v2 whole, which is shorter than its diff:
```python
import functools

import jax
import jax.numpy as jnp
from jax import lax
from jax.experimental import pallas as pl
from jax.experimental.pallas import tpu as pltpu
from jax.sharding import PartitionSpec as P

MESH = pl.DeviceIdType.MESH
NN = (((1,), (0,)), ((), ()))
NT = (((1,), (1,)), ((), ()))
TN = (((0,), (0,)), ((), ()))


def split(a):
    head = a.astype(jnp.bfloat16)
    return head, (a - head.astype(jnp.float32)).astype(jnp.bfloat16)


def fast(a, b, dims=NN):
    if dims == TN:
        a, dims = a.T, NN
    (ah, al), (bh, bl) = split(a), split(b)
    dot = functools.partial(
        lax.dot_general, dimension_numbers=dims, preferred_element_type=jnp.float32
    )
    return dot(ah, bh) + (dot(ah, bl) + dot(al, bh))


def pivoted(entries, lines):
    span = range(len(lines))
    for j in span:
        scale = 1.0 / entries[j][j]
        lines[j] = lines[j] * scale
        scaled = [entries[j][q] * scale if q > j else None for q in span]
        for i in span:
            if i == j:
                continue
            factor = entries[min(i, j)][max(i, j)]
            for q in range(max(i, j + 1), len(lines)):
                entries[i][q] = entries[i][q] - factor * scaled[q]
            lines[i] = lines[i] - factor * lines[j]
        entries[j] = scaled
    return lines


def first_row(values, i):
    return pltpu.roll(values, values.shape[0] - i, 0)[0:1] if i else values[0:1]


def inverted(columns):
    span = range(len(columns))
    shape = (len(columns), 128)
    rows = lax.broadcasted_iota(jnp.int32, shape, 0)
    lanes = lax.broadcasted_iota(jnp.int32, (1, shape[1]), 1)
    wide = [jnp.broadcast_to(column, shape) for column in columns]
    entries = [[first_row(wide[q], i) if q >= i else None for q in span] for i in span]
    lines = pivoted(entries, [(lanes == i).astype(jnp.float32) for i in span])
    merged = jnp.broadcast_to(lines[0], shape)
    for i in span[1:]:
        merged = jnp.where(rows == i, jnp.broadcast_to(lines[i], shape), merged)
    return merged


def eliminate(system, size, block=8):
    width = system.shape[1]
    shape = (block, width)
    rows = lax.broadcasted_iota(jnp.int32, shape, 0)
    panels = [system[p : p + block] for p in range(0, system.shape[0], block)]
    span = range(block)
    for k in range(0, size, block):
        pivot = panels[k // block]
        lines = [first_row(pivot, i) for i in span]
        entries = [
            [jnp.broadcast_to(lines[i][:, k + q : k + q + 1], (1, width)) if q >= i else None for q in span]
            for i in span
        ]
        columns = [
            [jnp.broadcast_to(panel[:, k + q : k + q + 1], shape) for q in span]
            for panel in panels
            if panel is not pivot
        ]
        lines = pivoted(entries, lines)
        lines = [jnp.broadcast_to(line, shape) for line in lines]
        merged = lines[0]
        for j in span[1:]:
            merged = jnp.where(rows == j, lines[j], merged)
        others = iter(columns)
        updated = []
        for panel in panels:
            if panel is pivot:
                updated.append(merged)
                continue
            column = next(others)
            update = column[0] * lines[0]
            for j in span[1:]:
                update = update + column[j] * lines[j]
            updated.append(panel - update)
        panels = updated
    return jnp.concatenate(panels, axis=0)[:, size:]


def identity(size):
    return (
        lax.broadcasted_iota(jnp.int32, (size, size), 0)
        == lax.broadcasted_iota(jnp.int32, (size, size), 1)
    ).astype(jnp.float32)


def packed(gram, width):
    groups = max(1, width // gram.shape[1])
    depth = gram.shape[0] // groups
    return jnp.concatenate([gram[g * depth : (g + 1) * depth] for g in range(groups)], axis=1)


def unpacked(tile, size):
    groups = max(1, tile.shape[1] // size)
    return jnp.concatenate([tile[:, g * size : (g + 1) * size] for g in range(groups)], axis=0)


def terms_of(left, right):
    total = left[:, 0:1] * right[0:1, :]
    for m in range(1, right.shape[0]):
        total = total + left[:, m : m + 1] * right[m : m + 1, :]
    return total


def thrice_rows(a):
    head = a.astype(jnp.bfloat16).astype(jnp.float32)
    return jnp.concatenate([head, head, a - head], axis=0)


def left_of(a):
    return thrice_rows(a).T.astype(jnp.bfloat16)


def right_of(a):
    head, tail = split(a)
    return jnp.concatenate([head, tail, head], axis=0)


def dot(a, b):
    return jnp.dot(a, b, preferred_element_type=jnp.float32)


def kernel(
    extents,
    operator_hbm,
    load_hbm,
    modes_hbm,
    coarse_hbm,
    count_hbm,
    maps_hbm,
    multipliers_ref,
    residual_ref,
    raw,
    load_ref,
    modes_ref,
    coarse_ref,
    maps_ref,
    count_ref,
    ordered,
    own_modes,
    all_modes,
    padded_load,
    probes,
    first_out,
    first_in,
    value_out,
    value_in,
    tile_out,
    tile_in,
    pair_out,
    pair_in,
    load_in,
    plane_sums,
    line_sums,
    raw_sem,
    first_send,
    first_recv,
    value_send,
    value_recv,
    tile_send,
    tile_recv,
    pair_send,
    pair_recv,
    load_send,
    load_recv,
    plane_send,
    plane_recv,
    line_send,
    line_recv,
):
    nx, ny, nz = extents
    cases = load_hbm.shape[0]
    width = load_hbm.shape[1] // 3
    modes = modes_hbm.shape[0]
    padded = own_modes.shape[0]
    here = (lax.axis_index("gx"), lax.axis_index("gy"), lax.axis_index("gz"))
    ix, iy, iz = here
    plane = nx * ny
    slot = ix * ny + iy

    fetches = [
        pltpu.make_async_copy(source, target, raw_sem.at[i])
        for i, (source, target) in enumerate(
            (
                (modes_hbm, modes_ref),
                (count_hbm, count_ref),
                (coarse_hbm, coarse_ref),
                (maps_hbm, maps_ref),
                (load_hbm, load_ref),
                (operator_hbm, raw),
            )
        )
    ]
    for fetch in fetches:
        fetch.start()

    def plane_peer(offset):
        other = lax.rem(slot + offset, plane)
        return (lax.div(other, ny), lax.rem(other, ny), iz)

    def line_peers():
        for turn in range(ny):
            for offset in range(1, nz):
                yield (ix, lax.rem(iy + turn, ny), lax.rem(iz + offset, nz))

    exists = []
    neighbour = []
    for d in range(3):
        exists.append(here[d] > 0)
        exists.append(here[d] < extents[d] - 1)
        for step in (-1, 1):
            neighbour.append(tuple(here[a] + (step if a == d else 0) for a in range(3)))
    flags = [jnp.where(e, 1, 0).astype(jnp.int32) for e in exists]

    def moved(position, f):
        return tuple(position[a] + ((2 * (f % 2) - 1) if a == f // 2 else 0) for a in range(3))

    def both_exist(f, g):
        if f != g:
            return jnp.logical_and(exists[f], exists[g])
        if f % 2:
            return here[f // 2] < extents[f // 2] - 2
        return here[f // 2] > 1

    pairs = [
        (f, g)
        for f in range(6)
        for g in range(6)
        if (f == g or f // 2 < g // 2) and extents[f // 2] > 1 + (f == g) and extents[g // 2] > 1
    ]

    first_in[...] = jnp.zeros(first_in.shape, jnp.float32)
    pair_in[...] = jnp.zeros(pair_in.shape, jnp.float32)
    tile_in[...] = jnp.zeros(tile_in.shape, jnp.float32)

    barrier = pltpu.get_barrier_semaphore()
    def greet(peer):
        pl.semaphore_signal(barrier, inc=1, device_id=peer, device_id_type=MESH)

    expected = 0
    for f in range(6):
        pl.when(exists[f])(functools.partial(greet, neighbour[f]))
        expected = expected + flags[f]
    if max(nx, nz) + ny > 6:
        for f, g in pairs:
            pl.when(both_exist(f, g))(functools.partial(greet, moved(moved(here, f), g)))
            expected = expected + jnp.where(both_exist(f, g), 1, 0).astype(jnp.int32)
        for offset in range(1, plane):
            greet(plane_peer(offset))
        for peer in line_peers():
            greet(peer)
        expected = expected + (plane - 1 + ny * (nz - 1))

    all_modes[...] = jnp.zeros(all_modes.shape, jnp.float32)
    probes[...] = jnp.zeros(probes.shape, jnp.float32)
    own_modes[...] = jnp.zeros(own_modes.shape, jnp.float32)
    padded_load[...] = jnp.zeros(padded_load.shape, jnp.float32)

    def face(values, f):
        return values[:, f * width : (f + 1) * width]

    def masked(values, f):
        return jnp.where(jnp.full(values.shape, flags[f], jnp.int32) == 1, values, 0.0)

    def block(values, f):
        return values[f * padded : (f + 1) * padded]

    def remote(source, target, send, recv, where):
        return pltpu.make_async_remote_copy(
            src_ref=source,
            dst_ref=target,
            send_sem=send,
            recv_sem=recv,
            device_id=where,
            device_id_type=MESH,
        )

    def owned(values):
        return jnp.concatenate([face(values, 1), face(values, 3), face(values, 5)], axis=1)

    sends = []

    def start_if(condition, copy):
        pl.when(condition)(copy.start)
        sends.append((condition, copy))

    for fetch in fetches[:5]:
        fetch.wait()

    def counted(shape):
        return jnp.broadcast_to(count_ref[...], shape)

    lines = lax.broadcasted_iota(jnp.int32, (width, width), 0)
    narrow = [(lines == maps_ref[d]).astype(jnp.float32).astype(jnp.bfloat16) for d in range(3)]
    for m in range(modes):
        own_modes[m : m + 1, :] = modes_ref[m]
        padded_load[m : m + 1, 0:cases] = coarse_ref[m]
    raw_modes = jnp.where(
        lax.broadcasted_iota(jnp.int32, own_modes.shape, 0) < counted(own_modes.shape), own_modes[...], 0.0
    )
    raw_modes = jnp.concatenate([masked(face(raw_modes, f), f) for f in range(6)], axis=1)
    exact = []
    rest = raw_modes
    for _ in range(3):
        exact.append(rest.astype(jnp.bfloat16).astype(jnp.float32))
        rest = rest - exact[-1]
    exact = jnp.concatenate(exact, axis=0).astype(jnp.bfloat16)
    pieces = []
    for d in range(3):
        found = lax.dot_general(face(exact, 2 * d), narrow[d], NT, preferred_element_type=jnp.float32)
        pieces.append(found[0:padded] + found[padded : 2 * padded] + found[2 * padded :])
        pieces.append(face(raw_modes, 2 * d + 1))
    mode_rows = jnp.concatenate(pieces, axis=1)
    mode_index = lax.broadcasted_iota(jnp.int32, (padded, 1), 0)
    inactive = mode_index >= counted((padded, 1))
    columns = []
    for m in range(padded):
        column = jnp.sum(raw_modes * raw_modes[m : m + 1], axis=1, keepdims=True)
        columns.append(column + jnp.where(jnp.logical_and(inactive, mode_index == m), 1.0, 0.0))
    active_load = jnp.where(
        lax.broadcasted_iota(jnp.int32, padded_load.shape, 0) < counted(padded_load.shape), padded_load[...], 0.0
    )
    load_rows = active_load.T[0:cases]
    coarse_inverse = inverted(columns)
    inverse_modes = terms_of(coarse_inverse, mode_rows)
    spread = terms_of(load_rows, inverse_modes)
    for f in range(6):
        value_out[0, f] = face(spread, f)
        first_out[f, 0:padded, :] = -face(mode_rows, f)
        first_out[f, padded:, :] = face(inverse_modes, f)

    pl.semaphore_wait(barrier, expected)

    def value_copy(phase, f, landing):
        return remote(
            value_out.at[phase, f],
            value_in.at[phase, landing],
            value_send.at[phase, f],
            value_recv.at[phase, landing],
            neighbour[f],
        )

    def first_copy(f, landing):
        return remote(first_out.at[f], first_in.at[landing], first_send.at[f], first_recv.at[landing], neighbour[f])

    def load_copy(d, f):
        return remote(
            load_ref.at[:, pl.ds(d * width, width)],
            load_in.at[d],
            load_send.at[d],
            load_recv.at[d],
            neighbour[f],
        )

    def tile_copy(phase, f, landing):
        return remote(
            tile_out.at[phase, f],
            tile_in.at[phase, landing],
            tile_send.at[phase, f],
            tile_recv.at[phase, landing],
            neighbour[f],
        )

    def pair_copy(phase, index, landing):
        f, g = pairs[index]
        return remote(
            pair_out.at[phase, index],
            pair_in.at[phase, landing],
            pair_send.at[phase, index],
            pair_recv.at[phase, landing],
            moved(moved(here, f), g),
        )

    def send_values(phase):
        odd = lax.rem(ix, 2) == 1
        even = jnp.logical_not(odd)
        copies = [value_copy(phase, f, f ^ 1) for f in range(6)]
        start_if(jnp.logical_and(exists[1], odd), copies[1])
        start_if(jnp.logical_and(exists[0], even), copies[0])
        start_if(jnp.logical_and(exists[0], odd), copies[0])
        start_if(jnp.logical_and(exists[1], even), copies[1])
        for f in (4, 5, 2, 3):
            start_if(exists[f], copies[f])

    def wait_values(phase):
        for f in range(6):
            pl.when(exists[f])(value_copy(phase, f, f).wait_recv)

    def send_coefficients(phase, share, found):
        gap = jnp.zeros((padded, width - cases), jnp.float32)
        low = [jnp.concatenate([block(found, f), gap], axis=1) for f in range(6)]
        gap = jnp.zeros((padded, width - 2 * cases), jnp.float32)
        for f in range(6):
            tile_out[phase, f] = jnp.concatenate([share, block(found, f), gap], axis=1)
        for index, (f, g) in enumerate(pairs):
            if f == g:
                pair_out[phase, index] = low[f]
            else:
                pair_out[phase, index] = jnp.concatenate([block(found, f), block(found, g), gap], axis=1)
        def near(index):
            f, g = pairs[index]
            return 2 <= f < 4 or 2 <= g < 4

        def start_pairs(chosen):
            for index in chosen:
                f, g = pairs[index]
                start_if(both_exist(f, g), pair_copy(phase, index, pairs.index((f ^ 1, g ^ 1))))

        start_pairs([index for index in range(len(pairs)) if not near(index)])
        for f in range(6):
            start_if(exists[f], tile_copy(phase, f, f ^ 1))
        start_pairs([index for index in range(len(pairs)) if near(index)])

    def coefficients_of(phase, share, found, sign):
        for f in range(6):
            pl.when(exists[f])(tile_copy(phase, f, f).wait_recv)
        back = tile_in[phase, 0]
        for f in range(1, 6):
            back = back + tile_in[phase, f]
        every = [share - sign * back[:, cases : 2 * cases]]
        for index, (f, g) in enumerate(pairs):
            pl.when(both_exist(f, g))(pair_copy(phase, index, index).wait_recv)
        first = [None] * 6
        second = [None] * 6
        for index, (a, b) in enumerate(pairs):
            tile = pair_in[phase, index]
            first[b] = tile if first[b] is None else first[b] + tile
            if a != b:
                second[a] = tile if second[a] is None else second[a] + tile
        for f in range(6):
            term = block(found, f)
            if first[f] is not None:
                term = term + first[f][:, 0:cases]
            if second[f] is not None:
                term = term + second[f][:, cases : 2 * cases]
            every.append(tile_in[phase, f][:, 0:cases] - sign * term)
        every.append(jnp.zeros((padded, cases), jnp.float32))
        return jnp.concatenate(every, axis=0)

    def assembled(phase):
        return jnp.concatenate(
            [masked(value_out[phase, f] - value_in[phase, f], f) for f in range(6)], axis=1
        )

    def applied(values):
        head, tail = split(values)
        both = dot(jnp.concatenate([head, tail], axis=0), ordered[...])
        half = values.shape[0]
        return both[0:half] + both[half:]

    send_values(0)
    for f in range(6):
        start_if(exists[f], first_copy(f, f ^ 1))
    for d in range(3):
        start_if(exists[2 * d + 1], load_copy(d, 2 * d + 1))

    all_modes[0:padded, :] = mode_rows
    probes[6 * padded : 7 * padded, :] = inverse_modes
    fetches[5].wait()
    for d in range(3):
        low = 2 * d * width
        raw[pl.ds(low, width), :] = dot(narrow[d], raw[pl.ds(low, width), :]).astype(jnp.bfloat16)
    for d in range(3):
        low = 2 * d * width
        ordered[:, low : low + width] = lax.dot_general(
            raw[:, low : low + width], narrow[d], NT, preferred_element_type=jnp.float32
        ).astype(jnp.bfloat16)
        ordered[:, low + width : low + 2 * width] = raw[:, low + width : low + 2 * width]
    wait_values(0)
    for f in range(6):
        pl.when(exists[f])(first_copy(f, f).wait_recv)
    for f in range(6):
        span = slice(f * width, (f + 1) * width)
        all_modes[(1 + f) * padded : (2 + f) * padded, span] = first_in[f, 0:padded, :]
        probes[f * padded : (f + 1) * padded, span] = first_in[f, padded:, :]
    every_probe = split(probes[...])
    initial = assembled(0)
    product = applied(initial)
    for f in range(6):
        value_out[1, f] = face(product, f)
    send_values(1)
    for d in range(3):
        pl.when(exists[2 * d])(load_copy(d, 2 * d).wait_recv)
    right = []
    for d in range(3):
        right.append(masked(-load_in[d], 2 * d))
        right.append(masked(load_ref[:, d * width : (d + 1) * width], 2 * d + 1))
    right = jnp.concatenate(right, axis=1)
    found = fast(probes[...], product, NT)
    shares = fast(inverse_modes, right, NT) - block(found, 6)
    send_coefficients(0, shares, found)
    every_mode = all_modes[...]
    images = applied(jnp.concatenate([every_mode, probes[...]], axis=0))
    depth = every_mode.shape[0]
    probe_image = images[depth:]
    mode_image = images[0:depth]
    cross_image = fast(probe_image, every_mode, NT)
    mode_stack = right_of(every_mode)
    image_stack = right_of(mode_image)
    head, tail = split(cross_image)
    folds = jnp.concatenate([head, head, tail], axis=1)

    def preconditioned(values, image, coefficients):
        left = left_of(0.25 * coefficients)
        return values - dot(left, mode_stack), image - dot(left, image_stack)

    wait_values(1)
    residual = right - assembled(1)
    product = applied(residual)
    probed = fast(probe_image, residual, NT)
    coefficients = coefficients_of(0, shares, found, -1.0)
    start, product = preconditioned(residual, product, coefficients)
    for f in range(6):
        value_out[2, f] = face(product, f)
    send_values(2)
    found = probed - dot(folds, right_of(0.25 * coefficients))
    shares = block(found, 6)
    send_coefficients(1, shares, found)

    relay = ny - 1
    is_relay = iy == relay

    def gather_copy(which, offset):
        other = lax.rem(ix + offset, nx)
        return remote(
            plane_sums.at[which, slot],
            plane_sums.at[which, slot],
            plane_send.at[which, offset],
            plane_recv.at[which, slot],
            (other, relay, iz),
        )

    def spread_targets():
        for turn in range(ny):
            for offset in range(nz):
                if turn or offset:
                    yield turn * nz + offset, (lax.rem(relay + turn, ny), lax.rem(iz + offset, nz))

    def spread_copy(which, index, position):
        return remote(
            line_sums.at[which, iz],
            line_sums.at[which, iz],
            line_send.at[which, index],
            line_recv.at[which, iz],
            (ix, *position),
        )

    def sum_start(which, tile):
        plane_sums[which, slot] = tile
        for offset in range(nx):
            if offset:
                gather_copy(which, offset).start()
            else:
                pl.when(iy != relay)(gather_copy(which, offset).start)

    def sum_middle(which):
        @pl.when(is_relay)
        def _():
            for other in range(plane):
                copy = remote(
                    plane_sums.at[which, other],
                    plane_sums.at[which, other],
                    plane_send.at[which, 0],
                    plane_recv.at[which, other],
                    (ix, iy, iz),
                )
                pl.when(slot != other)(copy.wait_recv)
            total = plane_sums[which, 0]
            for other in range(1, plane):
                total = total + plane_sums[which, other]
            line_sums[which, iz] = total
            for index, position in spread_targets():
                spread_copy(which, index, position).start()

    def sum_end(which):
        for other in range(nz):
            copy = remote(
                line_sums.at[which, other],
                line_sums.at[which, other],
                line_send.at[which, 0],
                line_recv.at[which, other],
                (ix, iy, iz),
            )
            pl.when(jnp.logical_or(iy != relay, iz != other))(copy.wait_recv)
        total = line_sums[which, 0]
        for other in range(1, nz):
            total = total + line_sums[which, other]
        half = total.shape[0] // 2
        return unpacked(total[0:half], cases), unpacked(total[half:], cases)

    def sum_finish(which):
        for offset in range(nx):
            if offset:
                gather_copy(which, offset).wait_send()
            else:
                pl.when(iy != relay)(gather_copy(which, offset).wait_send)

        @pl.when(is_relay)
        def _():
            for index, position in spread_targets():
                spread_copy(which, index, position).wait_send()

    sum_start(
        0,
        jnp.concatenate(
            [
                packed(fast(owned(start), owned(residual), NT), width),
                packed(fast(start, product, NT), width),
            ],
            axis=0,
        ),
    )
    wait_values(2)
    image = assembled(2)
    product = applied(image)
    sum_middle(0)
    coefficients = coefficients_of(1, shares, found, 1.0)
    second, product = preconditioned(image, product, coefficients)
    sum_start(
        1,
        jnp.concatenate(
            [
                packed(fast(owned(second), owned(image), NT), width),
                packed(fast(second, product, NT), width),
            ],
            axis=0,
        ),
    )
    for f in range(6):
        value_out[3, f] = face(product, f)
    send_values(3)
    sum_middle(1)
    gram, energy = sum_end(0)
    inverse = eliminate(jnp.concatenate([energy, identity(cases)], axis=1), cases)
    alpha = fast(inverse, gram)
    starts = jnp.concatenate([owned(start), -owned(image)], axis=1)
    base = jnp.concatenate([owned(initial), owned(residual)], axis=1) + fast(alpha, starts, TN)
    wait_values(3)
    seconds = jnp.concatenate([owned(second), -owned(assembled(3))], axis=1)
    for condition, copy in sends:
        pl.when(condition)(copy.wait_send)
    sum_finish(0)
    cross, last = sum_end(1)
    carried = fast(inverse, cross)
    schur = last - fast(cross, carried)
    right_side = fast(cross, alpha) - energy
    tail = eliminate(jnp.concatenate([schur, right_side], axis=1), cases)
    steps = right_of(seconds - fast(carried, starts, TN))
    result = base - dot(left_of(tail), steps)
    multipliers_ref[...] = result[:, 0 : 3 * width]
    residual_ref[...] = result[:, 3 * width :]
    sum_finish(1)


def put_out(multipliers_ref, residual_ref, multipliers_hbm, residual_hbm, sem):
    copies = [
        pltpu.make_async_copy(multipliers_ref, multipliers_hbm, sem.at[0]),
        pltpu.make_async_copy(residual_ref, residual_hbm, sem.at[1]),
    ]
    for copy in copies:
        copy.start()
    for copy in copies:
        copy.wait()


def held(array):
    return pltpu.with_memory_space_constraint(array, pltpu.HBM)


def rows_apart(array):
    return jnp.swapaxes(array, 2, 3).reshape(array.shape[3], 1, array.shape[4])


def local(extents, dual_operators, dual_load, rigid_modes, coarse_load, mode_counts, face_maps):
    size = dual_operators.shape[-1]
    cases = dual_load.shape[-2]
    width = dual_load.shape[-1] // 3
    modes = rigid_modes.shape[-2]
    padded = -(-modes // 8) * 8
    nx, ny, nz = extents
    plane = nx * ny
    tile = 2 * cases // max(1, width // cases)
    f32 = jnp.float32
    vmem = pl.BlockSpec(memory_space=pltpu.VMEM)
    hbm = pl.BlockSpec(memory_space=pltpu.HBM)
    dma = pltpu.SemaphoreType.DMA
    out = jax.ShapeDtypeStruct((cases, 3 * width), f32)
    multipliers, residual = pl.pallas_call(
        functools.partial(kernel, extents),
        out_shape=(out, out),
        in_specs=[
            hbm,
            hbm,
            hbm,
            hbm,
            hbm,
            hbm,
        ],
        out_specs=(vmem, vmem),
        scratch_shapes=[
            pltpu.VMEM((size, size), dual_operators.dtype),
            pltpu.VMEM((cases, 3 * width), f32),
            pltpu.VMEM((modes, 1, size), f32),
            pltpu.VMEM((modes, 1, cases), f32),
            pltpu.VMEM((3, 1, width), jnp.int32),
            pltpu.VMEM((1, 1), jnp.int32),
            pltpu.VMEM((size, size), dual_operators.dtype),
            pltpu.VMEM((padded, size), f32),
            pltpu.VMEM((8 * padded, size), f32),
            pltpu.VMEM((padded, width), f32),
            pltpu.VMEM((8 * padded, size), f32),
            pltpu.VMEM((6, 2 * padded, width), f32),
            pltpu.VMEM((6, 2 * padded, width), f32),
            pltpu.VMEM((4, 6, cases, width), f32),
            pltpu.VMEM((4, 6, cases, width), f32),
            pltpu.VMEM((2, 6, padded, width), f32),
            pltpu.VMEM((2, 6, padded, width), f32),
            pltpu.VMEM((2, 18, padded, width), f32),
            pltpu.VMEM((2, 18, padded, width), f32),
            pltpu.VMEM((3, cases, width), f32),
            pltpu.VMEM((2, plane, tile, width), f32),
            pltpu.VMEM((2, nz, tile, width), f32),
            dma((6,)),
            dma((6,)),
            dma((6,)),
            dma((4, 6)),
            dma((4, 6)),
            dma((2, 6)),
            dma((2, 6)),
            dma((2, 18)),
            dma((2, 18)),
            dma((3,)),
            dma((3,)),
            dma((2, nx)),
            dma((2, plane)),
            dma((2, ny * nz)),
            dma((2, nz)),
        ],
        compiler_params=pltpu.CompilerParams(collective_id=0, has_side_effects=True, vmem_limit_bytes=16 * 1024 * 1024
        ),
    )(
        held(dual_operators.reshape(size, size)),
        held(dual_load.reshape(cases, 3 * width)),
        held(rows_apart(rigid_modes)),
        held(rows_apart(coarse_load)),
        mode_counts.reshape(1, 1),
        held(rows_apart(face_maps)),
    )
    multipliers, residual = pl.pallas_call(
        put_out,
        out_shape=(out, out),
        in_specs=[vmem, vmem],
        out_specs=(hbm, hbm),
        scratch_shapes=[dma((2,))],
        compiler_params=pltpu.CompilerParams(vmem_limit_bytes=1024 * 1024),
    )(multipliers, residual)
    shape = (1, 1, 1, cases, 3 * width)
    return multipliers.reshape(shape), residual.reshape(shape)


def solution(mesh):
    extents = (mesh.shape["gx"], mesh.shape["gy"], mesh.shape["gz"])
    spec = P("gx", "gy", "gz", None, None)
    return jax.shard_map(
        functools.partial(local, extents),
        mesh=mesh,
        in_specs=(spec, spec, spec, spec, P("gx", "gy", "gz"), spec),
        out_specs=(spec, spec),
        check_vma=False,
    )
```

time: 30.7 us -> 28.9 us (0.941)
  Pallas kernels: 29.3 us -> 27.5 us
    pallas_call x1, Pallas kernels: 28.6 us -> 26.8 us  [local(): pl.pallas_call(functools.partial(kernel, extents), out_shape=(out, out),...]
where the time goes in v2:
time: 28.9 us; the launch traced here: 28.8 us
  Pallas kernels  27.5 us (95%)
  between operations  1.29 us (4%)
    pallas_call x1, Pallas kernels, local(): pl.pallas_call(functools.partial(kernel, extents), out_shape=(out, out),...  26.8 us
    pallas_call x1, Pallas kernels, local(): pl.pallas_call(put_out, out_shape=(out, out), in_specs=[vmem, vmem], out_...  0.66 us

profile of v2, /device:TPU:0, one launch (start us, length us, event | category | flops | bytes accessed | tf_op | source)
XLA Modules:
  0.0 28.8 jit_solution(18166153991885384319)
XLA Ops:
  1.3 26.8 %shard_map.77 = (f32[32,384]{1,0:T(8,128)S(1)}, f32[32,384]{1,0:T(8,128)S(1)}) custom-call(bf16[768,768]{1,0:T(8,128)(2,1)} %bitcast.9, f32[32,384]{1,0:T(8,128)} %bitcast.10, f32[6,1,768]{2,1,0:T(1,128)} %bitcast.11, f32[6,1,32]{2,1,0:T(1,128)} %bitcast.12, s32[1,1]{1,0:T(1,128)} %bitcast.8.count_hbm, s32[3,1,128]{2,1,0:T(1,128)} %bitcast.13), custom_call_target="tpu_custom_call" | custom-call | tf_op jit(solution)/shard_map/pallas_call | solution.py:712
  28.1 0.7 %shard_map.78 = (f32[32,384]{1,0:T(8,128)}, f32[32,384]{1,0:T(8,128)}) custom-call(f32[32,384]{1,0:T(8,128)S(1)} %get-tuple-element.6.multipliers_ref, f32[32,384]{1,0:T(8,128)S(1)} %get-tuple-element.7.residual_ref), custom_call_target="tpu_custom_call" | custom-call | tf_op jit(solution)/shard_map/pallas_call | solution.py:773

commit v3 on v2

--- a/solution.py
+++ b/solution.py
@@ -385,15 +385,33 @@
             neighbour[f],
         )
 
+    far = [f != g and f < 2 and g >= 4 for f, g in pairs]
+
+    def pair_part(ref, phase, index, wide):
+        return ref.at[phase, index] if wide else ref.at[phase, index, pl.ds(0, padded)]
+
     def pair_copy(phase, index, landing):
         f, g = pairs[index]
         return remote(
-            pair_out.at[phase, index],
-            pair_in.at[phase, landing],
+            pair_part(pair_out, phase, index, far[index]),
+            pair_part(pair_in, phase, landing, far[index]),
             pair_send.at[phase, index],
             pair_recv.at[phase, landing],
             moved(moved(here, f), g),
         )
+
+    def start_pairs(phase, chosen):
+        for index in chosen:
+            f, g = pairs[index]
+            start_if(both_exist(f, g), pair_copy(phase, index, pairs.index((f ^ 1, g ^ 1))))
+
+    def wait_pairs(phase, chosen):
+        for index in chosen:
+            f, g = pairs[index]
+            pl.when(both_exist(f, g))(pair_copy(phase, index, index).wait_recv)
+
+    far_pairs = [index for index in range(len(pairs)) if far[index]]
+    near_pairs = [index for index in range(len(pairs)) if not far[index]]
 
     def send_values(phase):
         odd = lax.rem(ix, 2) == 1
@@ -410,56 +428,57 @@
         for f in range(6):
             pl.when(exists[f])(value_copy(phase, f, f).wait_recv)
 
-    def send_coefficients(phase, share, found):
-        gap = jnp.zeros((padded, width - cases), jnp.float32)
-        low = [jnp.concatenate([block(found, f), gap], axis=1) for f in range(6)]
+    def send_far(phase, found):
+        for index in far_pairs:
+            f, g = pairs[index]
+            pair_out[phase, index, 0:padded, 0:cases] = block(found, f)
+            pair_out[phase, index, padded:, 0:cases] = block(found, g)
+        start_pairs(phase, far_pairs)
+
+    def send_near(phase, share, found):
         gap = jnp.zeros((padded, width - 2 * cases), jnp.float32)
         for f in range(6):
             tile_out[phase, f] = jnp.concatenate([share, block(found, f), gap], axis=1)
-        for index, (f, g) in enumerate(pairs):
-            if f == g:
-                pair_out[phase, index] = low[f]
-            else:
-                pair_out[phase, index] = jnp.concatenate([block(found, f), block(found, g), gap], axis=1)
-        def near(index):
-            f, g = pairs[index]
-            return 2 <= f < 4 or 2 <= g < 4
-
-        def start_pairs(chosen):
-            for index in chosen:
-                f, g = pairs[index]
-                start_if(both_exist(f, g), pair_copy(phase, index, pairs.index((f ^ 1, g ^ 1))))
-
-        start_pairs([index for index in range(len(pairs)) if not near(index)])
         for f in range(6):
             start_if(exists[f], tile_copy(phase, f, f ^ 1))
-        start_pairs([index for index in range(len(pairs)) if near(index)])
+        for index in near_pairs:
+            f, g = pairs[index]
+            if f == g:
+                pair_out[phase, index, 0:padded, 0:cases] = block(found, f)
+            else:
+                pair_out[phase, index, 0:padded, :] = jnp.concatenate([block(found, f), block(found, g), gap], axis=1)
+        start_pairs(phase, near_pairs)
 
     def coefficients_of(phase, share, found, sign):
         for f in range(6):
             pl.when(exists[f])(tile_copy(phase, f, f).wait_recv)
+        wait_pairs(phase, near_pairs)
         back = tile_in[phase, 0]
         for f in range(1, 6):
             back = back + tile_in[phase, f]
-        every = [share - sign * back[:, cases : 2 * cases]]
-        for index, (f, g) in enumerate(pairs):
-            pl.when(both_exist(f, g))(pair_copy(phase, index, index).wait_recv)
-        first = [None] * 6
-        second = [None] * 6
-        for index, (a, b) in enumerate(pairs):
-            tile = pair_in[phase, index]
-            first[b] = tile if first[b] is None else first[b] + tile
+        own = share - sign * back[:, cases : 2 * cases]
+        low = [None] * 6
+        high = [None] * 6
+        for index in near_pairs:
+            a, b = pairs[index]
+            tile = pair_in[phase, index, 0:padded]
+            low[b] = tile if low[b] is None else low[b] + tile
             if a != b:
-                second[a] = tile if second[a] is None else second[a] + tile
+                high[a] = tile if high[a] is None else high[a] + tile
+        terms = []
         for f in range(6):
             term = block(found, f)
-            if first[f] is not None:
-                term = term + first[f][:, 0:cases]
-            if second[f] is not None:
-                term = term + second[f][:, cases : 2 * cases]
-            every.append(tile_in[phase, f][:, 0:cases] - sign * term)
-        every.append(jnp.zeros((padded, cases), jnp.float32))
-        return jnp.concatenate(every, axis=0)
+            if low[f] is not None:
+                term = term + low[f][:, 0:cases]
+            if high[f] is not None:
+                term = term + high[f][:, cases : 2 * cases]
+            terms.append(tile_in[phase, f][:, 0:cases] - sign * term)
+        wait_pairs(phase, far_pairs)
+        for index in far_pairs:
+            a, b = pairs[index]
+            terms[b] = terms[b] - sign * pair_in[phase, index, 0:padded, 0:cases]
+            terms[a] = terms[a] - sign * pair_in[phase, index, padded:, 0:cases]
+        return jnp.concatenate([own, *terms, jnp.zeros((padded, cases), jnp.float32)], axis=0)
 
     def assembled(phase):
         return jnp.concatenate(
@@ -512,7 +531,8 @@
     right = jnp.concatenate(right, axis=1)
     found = fast(probes[...], product, NT)
     shares = fast(inverse_modes, right, NT) - block(found, 6)
-    send_coefficients(0, shares, found)
+    send_far(0, found)
+    send_near(0, shares, found)
     every_mode = all_modes[...]
     images = applied(jnp.concatenate([every_mode, probes[...]], axis=0))
     depth = every_mode.shape[0]
@@ -533,13 +553,14 @@
     product = applied(residual)
     probed = fast(probe_image, residual, NT)
     coefficients = coefficients_of(0, shares, found, -1.0)
+    found = probed - dot(folds, right_of(0.25 * coefficients))
+    send_far(1, found)
     start, product = preconditioned(residual, product, coefficients)
     for f in range(6):
         value_out[2, f] = face(product, f)
     send_values(2)
-    found = probed - dot(folds, right_of(0.25 * coefficients))
     shares = block(found, 6)
-    send_coefficients(1, shares, found)
+    send_near(1, shares, found)
 
     relay = ny - 1
     is_relay = iy == relay
@@ -637,7 +658,6 @@
     wait_values(2)
     image = assembled(2)
     product = applied(image)
-    sum_middle(0)
     coefficients = coefficients_of(1, shares, found, 1.0)
     second, product = preconditioned(image, product, coefficients)
     sum_start(
@@ -650,6 +670,7 @@
             axis=0,
         ),
     )
+    sum_middle(0)
     for f in range(6):
         value_out[3, f] = face(product, f)
     send_values(3)
@@ -739,8 +760,8 @@
             pltpu.VMEM((4, 6, cases, width), f32),
             pltpu.VMEM((2, 6, padded, width), f32),
             pltpu.VMEM((2, 6, padded, width), f32),
-            pltpu.VMEM((2, 18, padded, width), f32),
-            pltpu.VMEM((2, 18, padded, width), f32),
+            pltpu.VMEM((2, 18, 2 * padded, width), f32),
+            pltpu.VMEM((2, 18, 2 * padded, width), f32),
             pltpu.VMEM((3, cases, width), f32),
             pltpu.VMEM((2, plane, tile, width), f32),
             pltpu.VMEM((2, nz, tile, width), f32),

time: 28.9 us -> 28.9 us (level)
  no operation moved by 1% of the time
where the time goes in v3:
time: 28.9 us; the launch traced here: 28.7 us
  Pallas kernels  27.4 us (95%)
  between operations  1.29 us (4%)
    pallas_call x1, Pallas kernels, local(): pl.pallas_call(functools.partial(kernel, extents), out_shape=(out, out),...  26.8 us
    pallas_call x1, Pallas kernels, local(): pl.pallas_call(put_out, out_shape=(out, out), in_specs=[vmem, vmem], out_...  0.66 us

profile of v3, /device:TPU:0, one launch (start us, length us, event | category | flops | bytes accessed | tf_op | source)
XLA Modules:
  0.0 28.7 jit_solution(14023322845235313397)
XLA Ops:
  1.3 26.8 %shard_map.77 = (f32[32,384]{1,0:T(8,128)S(1)}, f32[32,384]{1,0:T(8,128)S(1)}) custom-call(bf16[768,768]{1,0:T(8,128)(2,1)} %bitcast.9, f32[32,384]{1,0:T(8,128)} %bitcast.10, f32[6,1,768]{2,1,0:T(1,128)} %bitcast.11, f32[6,1,32]{2,1,0:T(1,128)} %bitcast.12, s32[1,1]{1,0:T(1,128)} %bitcast.8.count_hbm, s32[3,1,128]{2,1,0:T(1,128)} %bitcast.13), custom_call_target="tpu_custom_call" | custom-call | tf_op jit(solution)/shard_map/pallas_call | solution.py:733
  28.1 0.7 %shard_map.78 = (f32[32,384]{1,0:T(8,128)}, f32[32,384]{1,0:T(8,128)}) custom-call(f32[32,384]{1,0:T(8,128)S(1)} %get-tuple-element.6.multipliers_ref, f32[32,384]{1,0:T(8,128)S(1)} %get-tuple-element.7.residual_ref), custom_call_target="tpu_custom_call" | custom-call | tf_op jit(solution)/shard_map/pallas_call | solution.py:794

commit v4 on v3

--- a/solution.py
+++ b/solution.py
@@ -413,16 +413,19 @@
     far_pairs = [index for index in range(len(pairs)) if far[index]]
     near_pairs = [index for index in range(len(pairs)) if not far[index]]
 
-    def send_values(phase):
+    def send_lines(phase):
         odd = lax.rem(ix, 2) == 1
         even = jnp.logical_not(odd)
-        copies = [value_copy(phase, f, f ^ 1) for f in range(6)]
-        start_if(jnp.logical_and(exists[1], odd), copies[1])
-        start_if(jnp.logical_and(exists[0], even), copies[0])
-        start_if(jnp.logical_and(exists[0], odd), copies[0])
-        start_if(jnp.logical_and(exists[1], even), copies[1])
+        for f, turn in ((1, odd), (0, even), (0, odd), (1, even)):
+            start_if(jnp.logical_and(exists[f], turn), value_copy(phase, f, f ^ 1))
+
+    def send_others(phase):
         for f in (4, 5, 2, 3):
-            start_if(exists[f], copies[f])
+            start_if(exists[f], value_copy(phase, f, f ^ 1))
+
+    def send_values(phase):
+        send_lines(phase)
+        send_others(phase)
 
     def wait_values(phase):
         for f in range(6):
@@ -554,49 +557,51 @@
     probed = fast(probe_image, residual, NT)
     coefficients = coefficients_of(0, shares, found, -1.0)
     found = probed - dot(folds, right_of(0.25 * coefficients))
-    send_far(1, found)
     start, product = preconditioned(residual, product, coefficients)
     for f in range(6):
         value_out[2, f] = face(product, f)
-    send_values(2)
+    send_lines(2)
+    send_far(1, found)
+    send_others(2)
     shares = block(found, 6)
     send_near(1, shares, found)
 
     relay = ny - 1
     is_relay = iy == relay
 
-    def gather_copy(which, offset):
-        other = lax.rem(ix + offset, nx)
-        return remote(
-            plane_sums.at[which, slot],
-            plane_sums.at[which, slot],
-            plane_send.at[which, offset],
-            plane_recv.at[which, slot],
-            (other, relay, iz),
-        )
-
-    def spread_targets():
-        for turn in range(ny):
+    def gathers(which, step):
+        for offset in range(nx):
+            other = lax.rem(nx - 1 - ix + offset, nx)
+            copy = remote(
+                plane_sums.at[which, slot],
+                plane_sums.at[which, slot],
+                plane_send.at[which, offset],
+                plane_recv.at[which, slot],
+                (other, relay, iz),
+            )
+            pl.when(jnp.logical_or(iy != relay, ix != other))(getattr(copy, step))
+
+    def spreads(which, step):
+        index = 0
+        for turn in range(1, ny + 1):
             for offset in range(nz):
-                if turn or offset:
-                    yield turn * nz + offset, (lax.rem(relay + turn, ny), lax.rem(iz + offset, nz))
-
-    def spread_copy(which, index, position):
-        return remote(
-            line_sums.at[which, iz],
-            line_sums.at[which, iz],
-            line_send.at[which, index],
-            line_recv.at[which, iz],
-            (ix, *position),
-        )
+                level = jnp.where(2 * iz < nz, nz - 1 - offset, offset)
+                copy = remote(
+                    line_sums.at[which, iz],
+                    line_sums.at[which, iz],
+                    line_send.at[which, index],
+                    line_recv.at[which, iz],
+                    (ix, lax.rem(relay + turn, ny), level),
+                )
+                if turn < ny:
+                    getattr(copy, step)()
+                else:
+                    pl.when(iz != level)(getattr(copy, step))
+                index = index + 1
 
     def sum_start(which, tile):
         plane_sums[which, slot] = tile
-        for offset in range(nx):
-            if offset:
-                gather_copy(which, offset).start()
-            else:
-                pl.when(iy != relay)(gather_copy(which, offset).start)
+        gathers(which, "start")
 
     def sum_middle(which):
         @pl.when(is_relay)
@@ -614,8 +619,7 @@
             for other in range(1, plane):
                 total = total + plane_sums[which, other]
             line_sums[which, iz] = total
-            for index, position in spread_targets():
-                spread_copy(which, index, position).start()
+            spreads(which, "start")
 
     def sum_end(which):
         for other in range(nz):
@@ -634,16 +638,8 @@
         return unpacked(total[0:half], cases), unpacked(total[half:], cases)
 
     def sum_finish(which):
-        for offset in range(nx):
-            if offset:
-                gather_copy(which, offset).wait_send()
-            else:
-                pl.when(iy != relay)(gather_copy(which, offset).wait_send)
-
-        @pl.when(is_relay)
-        def _():
-            for index, position in spread_targets():
-                spread_copy(which, index, position).wait_send()
+        gathers(which, "wait_send")
+        pl.when(is_relay)(functools.partial(spreads, which, "wait_send"))
 
     sum_start(
         0,

time: 28.9 us -> 28.5 us (0.986)
  Pallas kernels: 27.4 us -> 27.1 us
    pallas_call x1, Pallas kernels: 26.8 us -> 26.4 us  [local(): pl.pallas_call(functools.partial(kernel, extents), out_shape=(out, out),...]
where the time goes in v4:
time: 28.5 us; the launch traced here: 28.4 us
  Pallas kernels  27.1 us (95%)
  between operations  1.29 us (5%)
    pallas_call x1, Pallas kernels, local(): pl.pallas_call(functools.partial(kernel, extents), out_shape=(out, out),...  26.4 us
    pallas_call x1, Pallas kernels, local(): pl.pallas_call(put_out, out_shape=(out, out), in_specs=[vmem, vmem], out_...  0.66 us

profile of v4, /device:TPU:0, one launch (start us, length us, event | category | flops | bytes accessed | tf_op | source)
XLA Modules:
  0.0 28.4 jit_solution(7532451434345597372)
XLA Ops:
  1.3 26.4 %shard_map.77 = (f32[32,384]{1,0:T(8,128)S(1)}, f32[32,384]{1,0:T(8,128)S(1)}) custom-call(bf16[768,768]{1,0:T(8,128)(2,1)} %bitcast.9, f32[32,384]{1,0:T(8,128)} %bitcast.10, f32[6,1,768]{2,1,0:T(1,128)} %bitcast.11, f32[6,1,32]{2,1,0:T(1,128)} %bitcast.12, s32[1,1]{1,0:T(1,128)} %bitcast.8.count_hbm, s32[3,1,128]{2,1,0:T(1,128)} %bitcast.13), custom_call_target="tpu_custom_call" | custom-call | tf_op jit(solution)/shard_map/pallas_call | solution.py:729
  27.7 0.7 %shard_map.78 = (f32[32,384]{1,0:T(8,128)}, f32[32,384]{1,0:T(8,128)}) custom-call(f32[32,384]{1,0:T(8,128)S(1)} %get-tuple-element.6.multipliers_ref, f32[32,384]{1,0:T(8,128)S(1)} %get-tuple-element.7.residual_ref), custom_call_target="tpu_custom_call" | custom-call | tf_op jit(solution)/shard_map/pallas_call | solution.py:790

commit v5 on v4

--- a/solution.py
+++ b/solution.py
@@ -61,6 +61,13 @@
     for i in span[1:]:
         merged = jnp.where(rows == i, jnp.broadcast_to(lines[i], shape), merged)
     return merged
+
+
+def stacked(left, *right):
+    (head, tail), (first, second) = split(left), split(jnp.concatenate(right, axis=0))
+    dots = functools.partial(lax.dot_general, dimension_numbers=NT, preferred_element_type=jnp.float32)
+    both = dots(jnp.concatenate([head, tail], axis=0), first)
+    return both[0 : head.shape[0]] + (both[head.shape[0] :] + dots(head, second))
 
 
 def eliminate(system, size, block=8):
@@ -132,12 +139,16 @@
 
 
 def left_of(a):
-    return thrice_rows(a).T.astype(jnp.bfloat16)
+    return thrice_rows(a).astype(jnp.bfloat16)
 
 
 def right_of(a):
     head, tail = split(a)
     return jnp.concatenate([head, tail, head], axis=0)
+
+
+def dot_tn(a, b):
+    return lax.dot_general(a, b, TN, preferred_element_type=jnp.float32)
 
 
 def dot(a, b):
@@ -549,7 +560,7 @@
 
     def preconditioned(values, image, coefficients):
         left = left_of(0.25 * coefficients)
-        return values - dot(left, mode_stack), image - dot(left, image_stack)
+        return values - dot_tn(left, mode_stack), image - dot_tn(left, image_stack)
 
     wait_values(1)
     residual = right - assembled(1)
@@ -656,15 +667,12 @@
     product = applied(image)
     coefficients = coefficients_of(1, shares, found, 1.0)
     second, product = preconditioned(image, product, coefficients)
+    masked_image = jnp.concatenate(
+        [face(image, f) if f % 2 else jnp.zeros((cases, width), jnp.float32) for f in range(6)], axis=1
+    )
+    both = stacked(second, masked_image, product)
     sum_start(
-        1,
-        jnp.concatenate(
-            [
-                packed(fast(owned(second), owned(image), NT), width),
-                packed(fast(second, product, NT), width),
-            ],
-            axis=0,
-        ),
+        1, jnp.concatenate([packed(both[:, 0:cases], width), packed(both[:, cases:], width)], axis=0)
     )
     sum_middle(0)
     for f in range(6):
@@ -687,7 +695,7 @@
     right_side = fast(cross, alpha) - energy
     tail = eliminate(jnp.concatenate([schur, right_side], axis=1), cases)
     steps = right_of(seconds - fast(carried, starts, TN))
-    result = base - dot(left_of(tail), steps)
+    result = base - dot_tn(left_of(tail), steps)
     multipliers_ref[...] = result[:, 0 : 3 * width]
     residual_ref[...] = result[:, 3 * width :]
     sum_finish(1)

time: 28.5 us -> 28.5 us (level)
  no operation moved by 1% of the time
where the time goes in v5:
time: 28.5 us; the launch traced here: 28.3 us
  Pallas kernels  27 us (95%)
  between operations  1.29 us (5%)
    pallas_call x1, Pallas kernels, local(): pl.pallas_call(functools.partial(kernel, extents), out_shape=(out, out),...  26.4 us
    pallas_call x1, Pallas kernels, local(): pl.pallas_call(put_out, out_shape=(out, out), in_specs=[vmem, vmem], out_...  0.66 us

profile of v5, /device:TPU:0, one launch (start us, length us, event | category | flops | bytes accessed | tf_op | source)
XLA Modules:
  0.0 28.3 jit_solution(9822192642302781930)
XLA Ops:
  1.3 26.4 %shard_map.77 = (f32[32,384]{1,0:T(8,128)S(1)}, f32[32,384]{1,0:T(8,128)S(1)}) custom-call(bf16[768,768]{1,0:T(8,128)(2,1)} %bitcast.9, f32[32,384]{1,0:T(8,128)} %bitcast.10, f32[6,1,768]{2,1,0:T(1,128)} %bitcast.11, f32[6,1,32]{2,1,0:T(1,128)} %bitcast.12, s32[1,1]{1,0:T(1,128)} %bitcast.8.count_hbm, s32[3,1,128]{2,1,0:T(1,128)} %bitcast.13), custom_call_target="tpu_custom_call" | custom-call | tf_op jit(solution)/shard_map/pallas_call | solution.py:737
  27.6 0.7 %shard_map.78 = (f32[32,384]{1,0:T(8,128)}, f32[32,384]{1,0:T(8,128)}) custom-call(f32[32,384]{1,0:T(8,128)S(1)} %get-tuple-element.6.multipliers_ref, f32[32,384]{1,0:T(8,128)S(1)} %get-tuple-element.7.residual_ref), custom_call_target="tpu_custom_call" | custom-call | tf_op jit(solution)/shard_map/pallas_call | solution.py:798
